TPU v7x, 32 devices: a whole 2x2x4 slice. The times are simulated.
32 devices in a mesh: dp: 8 (over z, y), mp: 2 (over core), fsdp: 2 (over x).
Axes of the slice: x: 2, y: 2, z: 4, core: 2. Of those that a mesh axis runs over, the one named last changes fastest.
Arguments:
- features: bfloat16 [5, 1024, 512], P(None, ('dp', 'fsdp')), may hold values from -6 to 6
- memory_bank: bfloat16 [512, 32, 1024], P(('dp', 'fsdp')), may hold values from -1 to 1
- memory_fill: int32 [512], P(('dp', 'fsdp')), may hold values from 0 to 32
- left_keys: bfloat16 [512, 64, 1024], P(('dp', 'fsdp'), None, 'mp'), may hold values from -400 to 400
- left_values: bfloat16 [512, 64, 1024], P(('dp', 'fsdp'), None, 'mp'), may hold values from -6 to 6
- left_length: int32 [512], P(('dp', 'fsdp')), may hold values from 0 to 64
- w_query: bfloat16 [1024, 1024], P('fsdp', 'mp'), may hold values from -0.1875 to 0.1875
- w_key: bfloat16 [1024, 1024], P('fsdp', 'mp'), may hold values from -0.1875 to 0.1875
- w_value: bfloat16 [1024, 1024], P('fsdp', 'mp'), may hold values from -0.1875 to 0.1875
- w_out: bfloat16 [1024, 1024], P('mp', 'fsdp'), may hold values from -0.1875 to 0.1875
- w_up: bfloat16 [1024, 4096], P('fsdp', 'mp'), may hold values from -0.1875 to 0.1875
- w_down: bfloat16 [4096, 1024], P('mp', 'fsdp'), may hold values from -0.09375 to 0.09375
- out_gain: float32 [1024], replicated, may hold values from 0.1 to 1.9
Outputs:
- layer_out: bfloat16 [512, 5, 1024], P(('dp', 'fsdp'))
- memory_next: bfloat16 [512, 1024], P(('dp', 'fsdp'))
- center_keys: bfloat16 [512, 4, 1024], P(('dp', 'fsdp'), None, 'mp')
- center_values: bfloat16 [512, 4, 1024], P(('dp', 'fsdp'), None, 'mp')
All inputs are finite; a program needn't handle non-finite values.
Results may differ from a plain program's by a relative error of at most 0.0095.
Values may be sent and summed in bfloat16 or wider, within the bound.
A program may use at most 128 MiB of HBM per device.

v0:
```python
import jax
import jax.numpy as jnp
from jax import lax
from jax.sharding import PartitionSpec as P

HD = 64
GROUP = 4


epsilon = 1e-05
masked_score = -1e30


def normalize(values):
    values = values.astype(jnp.float32)
    average = jnp.mean(values, axis=-1, keepdims=True)
    centred = values - average
    variance = jnp.mean(centred * centred, axis=-1, keepdims=True)
    return centred * lax.rsqrt(variance + epsilon)


def matmul(left, right):
    return jnp.dot(left, right, preferred_element_type=jnp.float32)


def shards(
    features,
    memory_bank,
    memory_fill,
    left_keys,
    left_values,
    left_length,
    w_query,
    w_key,
    w_value,
    w_out,
    w_up,
    w_down,
    out_gain,
):
    frames, width_dev, all_streams = features.shape
    streams, mem_slots, width = memory_bank.shape
    left_slots = left_keys.shape[1]
    head_cols = w_query.shape[1]
    head_count = head_cols // HD
    flattened = features.reshape(frames * width_dev, all_streams)
    n_dp = lax.axis_size("dp")
    n_fsdp = lax.axis_size("fsdp")
    arrived = lax.all_to_all(flattened, ("dp", "fsdp"), split_axis=1, concat_axis=0, tiled=True)
    arrived = arrived.reshape(n_dp * n_fsdp, frames, width_dev, streams)
    inputs = jnp.transpose(arrived, (3, 1, 0, 2)).reshape(streams, frames, width)
    normed = normalize(inputs).astype(jnp.bfloat16)
    summary = jnp.mean(normed[:, :GROUP, :].astype(jnp.float32), axis=1).astype(jnp.bfloat16)
    query_rows = jnp.concatenate([normed, summary[:, None, :]], axis=1).reshape(-1, width)
    key_rows = jnp.concatenate([normed.reshape(-1, width), memory_bank.reshape(-1, width)], axis=0)
    query_sums = matmul(query_rows, lax.all_gather(w_query, "fsdp", axis=0, tiled=True))
    key_sums = matmul(key_rows, lax.all_gather(w_key, "fsdp", axis=0, tiled=True))
    value_sums = matmul(key_rows, lax.all_gather(w_value, "fsdp", axis=0, tiled=True))
    query_proj = query_sums.astype(jnp.bfloat16)
    key_proj = key_sums.astype(jnp.bfloat16)
    value_proj = value_sums.astype(jnp.bfloat16)
    group_total = streams * frames
    query_h = query_proj.reshape(streams, frames + 1, head_count, HD)
    ckey_h = key_proj[:group_total].reshape(streams, frames, head_count, HD)
    cval_h = value_proj[:group_total].reshape(streams, frames, head_count, HD)
    mkey_h = key_proj[group_total:].reshape(streams, mem_slots, head_count, HD)
    mval_h = value_proj[group_total:].reshape(streams, mem_slots, head_count, HD)
    lkey_h = left_keys.reshape(streams, left_slots, head_count, HD)
    lval_h = left_values.reshape(streams, left_slots, head_count, HD)
    not_summary = jnp.arange(frames + 1, dtype=jnp.int32) < frames
    mem_ok = jnp.arange(mem_slots, dtype=jnp.int32)[None, :] >= (mem_slots - memory_fill)[:, None]
    mem_mask = mem_ok[:, None, None, :] & not_summary[None, None, :, None]
    left_ok = (
        jnp.arange(left_slots, dtype=jnp.int32)[None, :] >= (left_slots - left_length)[:, None]
    )
    left_mask = left_ok[:, None, None, :]
    scale = HD ** (-0.5)
    score_mem = (
        jnp.einsum("sqhd,skhd->shqk", query_h, mkey_h, preferred_element_type=jnp.float32) * scale
    )
    score_left = (
        jnp.einsum("sqhd,skhd->shqk", query_h, lkey_h, preferred_element_type=jnp.float32) * scale
    )
    score_group = (
        jnp.einsum("sqhd,skhd->shqk", query_h, ckey_h, preferred_element_type=jnp.float32) * scale
    )
    score_mem = jnp.where(mem_mask, score_mem, masked_score)
    score_left = jnp.where(left_mask, score_left, masked_score)
    top = jnp.maximum(
        jnp.maximum(
            jnp.max(score_mem, axis=-1, keepdims=True), jnp.max(score_left, axis=-1, keepdims=True)
        ),
        jnp.max(score_group, axis=-1, keepdims=True),
    )
    exp_mem = jnp.exp(score_mem - top)
    exp_left = jnp.exp(score_left - top)
    exp_group = jnp.exp(score_group - top)
    totals = (
        jnp.sum(exp_mem, axis=-1, keepdims=True)
        + jnp.sum(exp_left, axis=-1, keepdims=True)
        + jnp.sum(exp_group, axis=-1, keepdims=True)
    )
    prob_mem = (exp_mem / totals).astype(jnp.bfloat16)
    prob_left = (exp_left / totals).astype(jnp.bfloat16)
    prob_group = (exp_group / totals).astype(jnp.bfloat16)
    attended = jnp.einsum("shqk,skhd->sqhd", prob_mem, mval_h, preferred_element_type=jnp.float32)
    attended = attended + jnp.einsum(
        "shqk,skhd->sqhd", prob_left, lval_h, preferred_element_type=jnp.float32
    )
    attended = attended + jnp.einsum(
        "shqk,skhd->sqhd", prob_group, cval_h, preferred_element_type=jnp.float32
    )
    attended = attended.astype(jnp.bfloat16).reshape(streams * (frames + 1), head_cols)
    attn_part = matmul(attended, lax.all_gather(w_out, "fsdp", axis=1, tiled=True))
    attn_out = (
        lax.psum(attn_part.astype(jnp.bfloat16), "mp")
        .astype(jnp.float32)
        .reshape(streams, frames + 1, width)
    )
    memory_next = jnp.tanh(attn_out[:, frames, :]).astype(jnp.bfloat16)
    hidden_state = inputs.astype(jnp.float32) + attn_out[:, :frames, :]
    h_norm = normalize(hidden_state).astype(jnp.bfloat16).reshape(-1, width)
    halves = lax.all_to_all(h_norm, "fsdp", split_axis=1, concat_axis=0, tiled=True)
    up_sums = lax.psum_scatter(
        matmul(halves, w_up).astype(jnp.bfloat16), "fsdp", scatter_dimension=0, tiled=True
    ).astype(jnp.float32)
    hidden = jax.nn.gelu(up_sums, approximate=True).astype(jnp.bfloat16)
    down_all = matmul(lax.all_gather(hidden, "fsdp", axis=0, tiled=True), w_down)
    down_part = lax.all_to_all(
        down_all.astype(jnp.bfloat16), "fsdp", split_axis=0, concat_axis=1, tiled=True
    ).astype(down_all.dtype)
    down_proj = lax.psum(down_part.astype(jnp.bfloat16), "mp").astype(jnp.float32)
    layer_out = (
        (normalize(hidden_state.reshape(-1, width) + down_proj) * out_gain)
        .astype(jnp.bfloat16)
        .reshape(streams, frames, width)
    )
    center_keys = key_proj[:group_total].reshape(streams, frames, head_cols)[:, :GROUP, :]
    center_values = value_proj[:group_total].reshape(streams, frames, head_cols)[:, :GROUP, :]
    return (layer_out, memory_next, center_keys, center_values)


def solution(mesh):
    in_specs = (
        P(None, ("dp", "fsdp"), None),
        P(("dp", "fsdp"), None, None),
        P(("dp", "fsdp")),
        P(("dp", "fsdp"), None, "mp"),
        P(("dp", "fsdp"), None, "mp"),
        P(("dp", "fsdp")),
        P("fsdp", "mp"),
        P("fsdp", "mp"),
        P("fsdp", "mp"),
        P("mp", "fsdp"),
        P("fsdp", "mp"),
        P("mp", "fsdp"),
        P(),
    )
    out_specs = (
        P(("dp", "fsdp"), None, None),
        P(("dp", "fsdp"), None),
        P(("dp", "fsdp"), None, "mp"),
        P(("dp", "fsdp"), None, "mp"),
    )
    return jax.shard_map(shards, mesh=mesh, in_specs=in_specs, out_specs=out_specs, check_vma=False)
```

profile of v0, /device:TPU:0, one launch (start us, length us, event | category | flops | bytes accessed | tf_op | source)
XLA Modules:
  0.0 236.4 jit_solution(17857175718315085044)
XLA Ops:
  9.4 1.8 copy.120
  11.2 1.4 all_to_all.38
  12.6 8.3 %all-to-all-start = ((bf16[320,16,32]{0,2,1:T(8,128)(2,1)}), bf16[320,16,32]{0,2,1:T(8,128)(2,1)S(1)}, u32[]{:S(2)}, u32[]{:S(2)}) async-start(bf16[320,16,32]{0,2,1:T(8,128)(2,1)} %all_to_all.38), calls=%async_computation | async-start | bytes 786432 | tf_op jit(solution)/shard_map/all_to_all | solution.py:49
  21.6 6.2 %reshape.219 = bf16[32,64,8,64]{3,2,1,0:T(8,128)(2,1)} reshape(bf16[32,64,512]{2,1,0:T(8,128)(2,1)} %param.16) | data formatting | bytes 4194304 | tf_op jit(solution)/shard_map/reshape | solution.py:68
  27.8 6.2 %reshape.221 = bf16[32,64,8,64]{3,2,1,0:T(8,128)(2,1)} reshape(bf16[32,64,512]{2,1,0:T(8,128)(2,1)} %param.17) | data formatting | bytes 4194304 | tf_op jit(solution)/shard_map/reshape | solution.py:69
  34.2 1.7 reshape.233
  35.9 1.8 bitcast_reduce_fusion
  37.9 2.1 multiply_reduce_fusion
  40.1 3.6 %copy.121 = f32[32,5,16,64]{3,2,0,1:T(8,128)} copy(f32[32,5,16,64]{3,1,0,2:T(8,128)} %bitcast.51) | data formatting | bytes 1310720 | tf_op jit(solution)/shard_map/convert_element_type | solution.py:121
  43.7 1.9 copy.122
  45.7 1.8 reshape.230
  49.0 1.7 reshape.231
  51.6 3.4 %convolution_convert_fusion = bf16[1184,512]{1,0:T(8,128)(2,1)S(1)} fusion(bf16[1024,512]{1,0:T(8,128)(2,1)} %all-gather.10.cloned.1.call-done, bf16[1024,1024]{1,0:T(8,128)(2,1)} %bitcast.57, bf16[160,1024]{1,0:T(8,128)(2,1)} %multiply_convert_fusion.3), kind=kOutput, calls=%fused_computation.4 | convolution fusion | flops 1246969856 | bytes 4685824 | tf_op jit(solution)/shard_map/dot_general | solution.py:23
  55.7 1.0 slice.40
  56.7 3.9 %all-gather.8.cloned.1.call-done = bf16[1024,512]{1,0:T(8,128)(2,1)} async-done(((bf16[512,512]{1,0:T(8,128)(2,1)}), bf16[1024,512]{1,0:T(8,128)(2,1)}) %all-gather.8.cloned.1.call-update) | async-done | bytes 1048592 | tf_op jit(solution)/shard_map/all_gather | solution.py:56
  60.6 1.6 convolution_convert_fusion.5
  62.5 1.1 reshape.220
  63.6 3.9 %reshape.218 = bf16[32,32,8,64]{3,2,1,0:T(8,128)(2,1)} reshape(bf16[1024,512]{1,0:T(8,128)(2,1)} %slice.40) | data formatting | bytes 2097152 | tf_op jit(solution)/shard_map/reshape | solution.py:66
  68.1 3.8 %fusion.63 = (f32[32,8,6]{2,1,0:T(8,128)S(1)}, f32[32,8,6,32]{3,2,1,0:T(8,128)S(1)}) fusion(bf16[32,32,8,64]{3,2,1,0:T(8,128)(2,1)} %reshape.218, bf16[32,6,8,64]{3,2,1,0:T(8,128)(2,1)S(1)} %reshape.217, pred[32,6,32]{2,1,0:T(8,128)(4,1)S(1)} %broadcast_and_fusion), kind=kOutput, calls=%fused_computation.93 | convolution fusion | flops 6437376 | bytes 1454080 | tf_op jit(solution)/shard_map/sqhd,skhd->shqk/dot_general | solution.py:79
  71.8 2.4 fusion.64
  77.0 6.5 %all-gather.6.cloned.1.call-done = bf16[1024,512]{1,0:T(8,128)(2,1)} async-done(((bf16[512,512]{1,0:T(8,128)(2,1)}), bf16[1024,512]{1,0:T(8,128)(2,1)}) %all-gather.6.cloned.1.call-update) | async-done | bytes 1048592 | tf_op jit(solution)/shard_map/all_gather | solution.py:58
  83.5 3.4 %convolution_convert_fusion.1 = bf16[1184,512]{1,0:T(8,128)(2,1)S(1)} fusion(bf16[1024,512]{1,0:T(8,128)(2,1)} %all-gather.6.cloned.1.call-done, bf16[1024,1024]{1,0:T(8,128)(2,1)} %bitcast.58, bf16[160,1024]{1,0:T(8,128)(2,1)} %multiply_convert_fusion.3), kind=kOutput, calls=%fused_computation.5 | convolution fusion | flops 1246969856 | bytes 4685824 | tf_op jit(solution)/shard_map/dot_general | solution.py:23
  86.9 1.0 copy-done.14
  88.9 3.0 %convolution_bitcast_fusion = f32[32,6,8,64]{3,1,2,0:T(8,128)} fusion(f32[32,8,6,5]{2,3,1,0:T(8,128)} %copy-done.6, bf16[32,5,8,64]{3,2,1,0:T(8,128)(2,1)} %reshape.222, f32[32,8,6]{2,1,0:T(8,128)S(1)} %add_add_fusion, f32[32,8,6]{2,1,0:T(8,128)S(1)} %maximum_maximum_fusion), kind=kOutput, calls=%fused_computation.23 | convolution fusion | flops 1006080 | bytes 600064 | tf_op jit(solution)/shard_map/shqk,skhd->sqhd/dot_general | solution.py:110
  91.9 1.0 slice.38
  93.0 3.9 %reshape.215 = bf16[32,32,8,64]{3,2,1,0:T(8,128)(2,1)} reshape(bf16[1024,512]{1,0:T(8,128)(2,1)} %slice.38) | data formatting | bytes 2097152 | tf_op jit(solution)/shard_map/reshape | solution.py:67
  96.9 2.7 %fusion.8 = f32[32,6,8,64]{3,1,2,0:T(8,128)S(1)} fusion(bf16[32,32,8,64]{3,2,1,0:T(8,128)(2,1)} %reshape.215, f32[32,8,6,32]{3,2,1,0:T(8,128)} %copy-done.7, f32[32,8,6]{2,1,0:T(8,128)S(1)} %copy-done.17, f32[32,8,6]{2,1,0:T(8,128)S(1)} %maximum_maximum_fusion), kind=kOutput, calls=%fused_computation.17 | convolution fusion | flops 6438912 | bytes 1650688 | tf_op jit(solution)/shard_map/shqk,skhd->sqhd/dot_general | solution.py:106
  100.6 1.5 fusion.38
  102.4 3.8 %all-gather.12.cloned.1.call-done = bf16[512,1024]{1,0:T(8,128)(2,1)} async-done(((bf16[512,512]{1,0:T(8,128)(2,1)}), bf16[512,1024]{1,0:T(8,128)(2,1)}) %all-gather.12.cloned.1.call-update) | async-done | bytes 1048592 | tf_op jit(solution)/shard_map/all_gather | solution.py:114
  106.2 2.4 convolution_convert_fusion.3
  108.6 1.1 reshape.224
  110.8 18.5 %all-reduce.3.cloned.1.call-done = bf16[32,6,1024]{2,0,1:T(8,128)(2,1)} async-done(((bf16[32,6,1024]{2,0,1:T(8,128)(2,1)}), bf16[32,6,1024]{2,0,1:T(8,128)(2,1)}) %all-reduce.3.cloned.1.call-update) | async-done | bytes 393232 | tf_op jit(solution)/shard_map/psum | solution.py:116
  129.3 1.1 reshape.225
  132.8 1.0 copy.143
  133.8 9.1 %all_to_all.51 = bf16[160,2,512]{2,0,1:T(8,128)(2,1)S(1)} all-to-all(bf16[160,2,512]{2,0,1:T(8,128)(2,1)S(1)} %copy.143), channel_id=1, replica_groups=mesh['dp'=8,'mp'=2,'fsdp'=2] {'fsdp'}, dimensions={1} | all-to-all | bytes 655360 | tf_op jit(solution)/shard_map/all_to_all | solution.py:123
  142.9 2.0 convolution_convert_fusion.2
  145.2 23.3 %reduce-scatter.2.cloned.1.call-done = bf16[160,2048]{1,0:T(8,128)(2,1)} async-done(((bf16[320,2048]{1,0:T(8,128)(2,1)}), bf16[160,2048]{1,0:T(8,128)(2,1)}) %reduce-scatter.2.cloned.1.call-update) | async-done | bytes 655376 | tf_op jit(solution)/shard_map/reduce_scatter | solution.py:124
  168.5 2.4 %fusion.37 = bf16[160,2048]{1,0:T(8,128)(2,1)} fusion(bf16[160,2048]{1,0:T(8,128)(2,1)} %reduce-scatter.2.cloned.1.call-done), kind=kLoop, calls=%fused_computation.32 | loop fusion | flops 3276800 | bytes 1310720 | tf_op jit(solution)/shard_map/convert_element_type | solution.py:127
  171.0 24.3 %all-gather.14.cloned.1.call-done = bf16[320,2048]{1,0:T(8,128)(2,1)} async-done(((bf16[160,2048]{1,0:T(8,128)(2,1)}), bf16[320,2048]{1,0:T(8,128)(2,1)}) %all-gather.14.cloned.1.call-update) | async-done | bytes 1310736 | tf_op jit(solution)/shard_map/all_gather | solution.py:128
  195.3 2.8 %convolution_convert_fusion.4 = bf16[320,512]{1,0:T(8,128)(2,1)S(1)} fusion(bf16[320,2048]{1,0:T(8,128)(2,1)} %all-gather.14.cloned.1.call-done, bf16[2048,512]{1,0:T(8,128)(2,1)} %param.24), kind=kOutput, calls=%fused_computation.35 | convolution fusion | flops 671252480 | bytes 3735552 | tf_op jit(solution)/shard_map/dot_general | solution.py:23
  198.1 8.5 %all_to_all.52 = bf16[2,160,512]{2,1,0:T(8,128)(2,1)S(1)} all-to-all(bf16[2,160,512]{2,1,0:T(8,128)(2,1)S(1)} %bitcast.56), channel_id=1, replica_groups=mesh['dp'=8,'mp'=2,'fsdp'=2] {'fsdp'}, dimensions={0} | all-to-all | bytes 655360 | tf_op jit(solution)/shard_map/all_to_all | solution.py:129
  209.0 1.7 slice.45
  210.6 1.4 copy.141
  212.0 1.4 reshape.226
  213.4 1.6 fusion.58
  214.9 11.0 %all-reduce.5.cloned.1.call-done = bf16[160,1024]{1,0:T(8,128)(2,1)} async-done(((bf16[160,1024]{1,0:T(8,128)(2,1)}), bf16[160,1024]{1,0:T(8,128)(2,1)}) %all-reduce.5.cloned.1.call-update) | async-done | bytes 327696 | tf_op jit(solution)/shard_map/psum | solution.py:132
  225.9 1.2 fusion.55
  227.1 1.2 multiply_reduce_fusion.1
  (112 shorter events, 19.8 us)
Async XLA Ops:
  7.2 135.8 %copy-start = (bf16[512,2048]{1,0:T(8,128)(2,1)S(1)}, bf16[512,2048]{1,0:T(8,128)(2,1)}, u32[]{:S(2)}) copy-start(bf16[512,2048]{1,0:T(8,128)(2,1)} %param.23) | copy-start | bytes 6291460
  7.2 44.4 %all-gather.10.cloned.1.call-start = ((), (), s32[]{:S(2)}) async-start(), calls=%async_computation.6 | async-start | bytes 1572864 | tf_op jit(solution)/shard_map/all_gather | solution.py:57
  7.9 52.7 %all-gather.8.cloned.1.call-start = ((), (), s32[]{:S(2)}) async-start(), calls=%async_computation.5 | async-start | bytes 1572864 | tf_op jit(solution)/shard_map/all_gather | solution.py:56
  8.7 74.8 %all-gather.6.cloned.1.call-start = ((), (), s32[]{:S(2)}) async-start(), calls=%async_computation.4 | async-start | bytes 1572864 | tf_op jit(solution)/shard_map/all_gather | solution.py:58
  9.4 12.1 %copy-start.19 = (s32[32]{0:T(128)S(1)}, s32[32]{0:T(128)}, u32[]{:S(2)}) copy-start(s32[32]{0:T(128)} %param.15) | copy-start | bytes 388
  9.4 12.2 %copy-start.20 = (s32[32]{0:T(128)S(1)}, s32[32]{0:T(128)}, u32[]{:S(2)}) copy-start(s32[32]{0:T(128)} %param.18) | copy-start | bytes 388
  12.6 21.6 %all-to-all-start = ((bf16[320,16,32]{0,2,1:T(8,128)(2,1)}), bf16[320,16,32]{0,2,1:T(8,128)(2,1)S(1)}, u32[]{:S(2)}, u32[]{:S(2)}) async-start(bf16[320,16,32]{0,2,1:T(8,128)(2,1)} %all_to_all.38), calls=%async_computation | async-start | bytes 786432 | tf_op jit(solution)/shard_map/all_to_all | solution.py:49
  20.9 85.3 %all-gather.12.cloned.1.call-start = ((), (), s32[]{:S(2)}) async-start(), calls=%async_computation.7 | async-start | bytes 1572864 | tf_op jit(solution)/shard_map/all_gather | solution.py:114
  21.5 107.8 %all-reduce.3.cloned.1.call-start = ((), (), s32[]{:S(2)}) async-start(), calls=%async_computation.8 | async-start | bytes 786432 | tf_op jit(solution)/shard_map/psum | solution.py:116
  40.1 3.6 %copy-start.1 = (f32[16,5,64,32]{2,1,3,0:T(8,128)S(1)}, f32[16,5,64,32]{2,1,3,0:T(8,128)}, u32[]{:S(2)}) copy-start(f32[16,5,64,32]{2,1,3,0:T(8,128)} %reshape.233) | copy-start | bytes 1966084
  55.0 5.7 %copy-start.10 = (bf16[192,1024]{1,0:T(8,128)(2,1)S(1)}, bf16[192,1024]{1,0:T(8,128)(2,1)}, u32[]{:S(2)}) copy-start(bf16[192,1024]{1,0:T(8,128)(2,1)} %reshape.216) | copy-start | bytes 1179652
  67.5 4.3 %copy-start.2 = (bf16[32,64,8,64]{3,2,1,0:T(8,128)(2,1)S(1)}, bf16[32,64,8,64]{3,2,1,0:T(8,128)(2,1)}, u32[]{:S(2)}) copy-start(bf16[32,64,8,64]{3,2,1,0:T(8,128)(2,1)} %reshape.219) | copy-start | bytes 6291460
  68.0 8.5 %copy-start.6 = (f32[32,8,6,5]{2,3,1,0:T(8,128)}, f32[32,8,6,5]{2,3,1,0:T(8,128)S(1)}, u32[]{:S(2)}) copy-start(f32[32,8,6,5]{2,3,1,0:T(8,128)S(1)} %get-tuple-element.27) | copy-start | bytes 92164
  71.8 4.0 %copy-start.7 = (f32[32,8,6,32]{3,2,1,0:T(8,128)}, f32[32,8,6,32]{3,2,1,0:T(8,128)S(1)}, u32[]{:S(2)}) copy-start(f32[32,8,6,32]{3,2,1,0:T(8,128)S(1)} %get-tuple-element.29) | copy-start | bytes 589828
  74.2 1.0 copy-start.3
  86.9 1.0 copy-start.14
  87.9 4.0 %copy-start.12 = (bf16[160,512]{1,0:T(8,128)(2,1)}, bf16[160,512]{1,0:T(8,128)(2,1)S(1)}, u32[]{:S(2)}) copy-start(bf16[160,512]{1,0:T(8,128)(2,1)S(1)} %slice.42) | copy-start | bytes 491524
  88.9 3.0 %copy-start.16 = (f32[32,8,6]{2,1,0:T(8,128)}, f32[32,8,6]{2,1,0:T(8,128)S(1)}, u32[]{:S(2)}) copy-start(f32[32,8,6]{2,1,0:T(8,128)S(1)} %add_add_fusion) | copy-start | bytes 18436
  88.9 3.0 %copy-start.15 = (bf16[1184,512]{1,0:T(8,128)(2,1)S(1)}, bf16[1184,512]{1,0:T(8,128)(2,1)}, u32[]{:S(2)}) copy-start(bf16[1184,512]{1,0:T(8,128)(2,1)} %copy-done.14) | copy-start | bytes 3637252
  93.0 3.9 %copy-start.17 = (f32[32,8,6]{2,1,0:T(8,128)S(1)}, f32[32,8,6]{2,1,0:T(8,128)}, u32[]{:S(2)}) copy-start(f32[32,8,6]{2,1,0:T(8,128)} %copy-done.16) | copy-start | bytes 18436
  96.9 2.8 %copy-start.4 = (f32[32,8,6,64]{3,2,1,0:T(8,128)S(1)}, f32[32,8,6,64]{3,2,1,0:T(8,128)}, u32[]{:S(2)}) copy-start(f32[32,8,6,64]{3,2,1,0:T(8,128)} %copy-done.3) | copy-start | bytes 1179652
  96.9 3.5 %copy-start.5 = (bf16[32,64,8,64]{3,2,1,0:T(8,128)(2,1)S(1)}, bf16[32,64,8,64]{3,2,1,0:T(8,128)(2,1)}, u32[]{:S(2)}) copy-start(bf16[32,64,8,64]{3,2,1,0:T(8,128)(2,1)} %reshape.221) | copy-start | bytes 6291460
  96.9 3.7 %copy-start.21 = (f32[32,6,8,64]{3,1,2,0:T(8,128)S(1)}, f32[32,6,8,64]{3,1,2,0:T(8,128)}, u32[]{:S(2)}) copy-start(f32[32,6,8,64]{3,1,2,0:T(8,128)} %convolution_bitcast_fusion) | copy-start | bytes 1179652
  110.7 57.8 %reduce-scatter.2.cloned.1.call-start = ((), (), s32[]{:S(2)}) async-start(), calls=%async_computation.9 | async-start | bytes 1966080 | tf_op jit(solution)/shard_map/reduce_scatter | solution.py:124
  130.3 0.9 copy-start.8
  144.9 50.4 %all-gather.14.cloned.1.call-start = ((), (), s32[]{:S(2)}) async-start(), calls=%async_computation.10 | async-start | bytes 1966080 | tf_op jit(solution)/shard_map/all_gather | solution.py:128
  170.9 36.5 %copy-start.13 = (bf16[160,512]{1,0:T(8,128)(2,1)S(1)}, bf16[160,512]{1,0:T(8,128)(2,1)}, u32[]{:S(2)}) copy-start(bf16[160,512]{1,0:T(8,128)(2,1)} %copy-done.12) | copy-start | bytes 491524
  170.9 55.0 %all-reduce.5.cloned.1.call-start = ((), (), s32[]{:S(2)}) async-start(), calls=%async_computation.11 | async-start | bytes 655360 | tf_op jit(solution)/shard_map/psum | solution.py:132
  198.1 9.4 %copy-start.11 = (bf16[160,512]{1,0:T(8,128)(2,1)S(1)}, bf16[160,512]{1,0:T(8,128)(2,1)}, u32[]{:S(2)}) copy-start(bf16[160,512]{1,0:T(8,128)(2,1)} %slice.41) | copy-start | bytes 491524
  212.0 16.3 %copy-start.18 = (f32[1024]{0:T(1024)S(1)}, f32[1024]{0:T(1024)}, u32[]{:S(2)}) copy-start(f32[1024]{0:T(1024)} %param.25) | copy-start | bytes 12292
  225.9 2.4 %copy-start.9 = (bf16[160,1024]{1,0:T(8,128)(2,1)S(1)}, bf16[160,1024]{1,0:T(8,128)(2,1)}, u32[]{:S(2)}) copy-start(bf16[160,1024]{1,0:T(8,128)(2,1)} %all-reduce.5.cloned.1.call-done) | copy-start | bytes 983044
Sparse Core Ops, SparseCore 0:
  9.5 28.2 all-gather.9
  39.3 21.2 all-gather.7
  62.2 21.2 all-gather.5
  84.9 21.2 all-gather.11
  110.8 18.3 all-reduce.2
  145.0 23.4 reduce-scatter.1
  171.0 24.2 all-gather.13
  207.5 18.3 all-reduce.4
where the time goes:
time: 238 us; the launch traced here: 236 us
  waiting for transfers between devices  94 us (39%)
  local copies, waits for them, and re-layouts  56.7 us (24%)
  matrix products  29.4 us (12%)
  blocking collectives  17.6 us (7%)
  other arithmetic  15.2 us (6%)
  between operations  14.6 us (6%)
  starting transfers between devices  8.88 us (4%)
    all_gather x1, waiting for transfers between devices, shards(): lax.all_gather(hidden, 'fsdp', axis=0, tiled=True)  24.3 us
    reduce_scatter x1, waiting for transfers between devices, shards(): lax.psum_scatter(matmul(halves, w_up).astype(jnp.bfloat16), 'fsdp', scatt...  23.3 us
    psum x1, waiting for transfers between devices, shards(): lax.psum(attn_part.astype(jnp.bfloat16), 'mp').astype(jnp.float32)  18.5 us
    dot_general x6, matrix products, matmul(): return jnp.dot(left, right, preferred_element_type=jnp.float32)  15.5 us
    psum x1, waiting for transfers between devices, shards(): lax.psum(down_part.astype(jnp.bfloat16), 'mp').astype(jnp.float32)  11 us
    convert_element_type x5, local copies, waits for them, and re-layouts, shards(): hidden_state = inputs.astype(jnp.float32) + attn_out[:, :frames, :]  10.6 us
    all_to_all x1, blocking collectives, shards(): lax.all_to_all(h_norm, 'fsdp', split_axis=1, concat_axis=0, tiled=True)  9.13 us
    all_to_all x1, blocking collectives, shards(): lax.all_to_all(down_all.astype(jnp.bfloat16), 'fsdp', split_axis=0, conca...  8.51 us
  transfers between devices with their start and end apart: 9, of which 7 were waited for; matrix products, arithmetic and copies ran while one was open for 32% of the time, Pallas kernels for 0%

commit v1 on v0

v1 whole, which is shorter than its diff:
```python
import functools

import jax
import jax.numpy as jnp
from jax import lax
from jax.experimental import pallas as pl
from jax.experimental.pallas import tpu as pltpu
from jax.sharding import PartitionSpec as P

HD = 64
GROUP = 4
ROWS = 8
KEYS = 128

epsilon = 1e-05
masked_score = -1e30
MESH = pl.DeviceIdType.MESH
bf16 = jnp.bfloat16
f32 = jnp.float32


def normalize(values):
    average = jnp.mean(values, axis=-1, keepdims=True)
    centred = values - average
    variance = jnp.mean(centred * centred, axis=-1, keepdims=True)
    return centred * lax.rsqrt(variance + epsilon)


def matmul(left, right):
    return jnp.dot(left, right, preferred_element_type=f32)


def body(
    frames,
    mem_slots,
    left_slots,
    x_ref,
    bias_ref,
    gain_ref,
    mem_hbm,
    lk_hbm,
    lv_hbm,
    wq_hbm,
    wk_hbm,
    wv_hbm,
    wo_hbm,
    wu_hbm,
    wd_hbm,
    out_ref,
    mnext_ref,
    ck_ref,
    cv_ref,
    far,
    own,
    mem_v,
    lk_v,
    lv_v,
    mk,
    mv,
    gk,
    gv,
    qs,
    rows_v,
    att,
    hid,
    hbuf,
    dacc,
    part,
    peer,
    send_sem,
    recv_sem,
    psend_sem,
    precv_sem,
    load_sem,
):
    d = lax.axis_index("dp")
    m = lax.axis_index("mp")
    f = lax.axis_index("fsdp")
    total, width = x_ref.shape
    streams = total // ROWS
    n_blocks, depth, cols = far.shape
    n_ff = (n_blocks - 4) // 2
    quarter = depth // 4
    c1 = quarter // 4
    c2 = (quarter - c1) // 2
    ybit = lax.rem(d, 2)
    zbit = lax.rem(lax.div(d, 2), 2)
    p = lax.rem(d, 4)
    py = p + 1 - 2 * ybit
    pz = p + 2 - 4 * zbit
    pd = 3 - p
    xdev = (d, m, 1 - f)
    ydev = (d + 1 - 2 * ybit, m, f)
    zdev = (d + 2 - 4 * zbit, m, f)
    mdev = (d, 1 - m, f)

    def own_hbm(b, start, size):
        r = pl.ds(pl.multiple_of(start, 16), size)
        if b < 4:
            return (wk_hbm, wv_hbm, wq_hbm, wo_hbm)[b].at[r, :]
        j = (b - 4) // 2
        if b % 2 == 0:
            return wu_hbm.at[r, pl.ds(j * cols, cols)]
        return wd_hbm.at[pl.ds(pl.multiple_of(start + j * depth, 16), size), :]

    def piece(b, start, size):
        return far.at[b, pl.ds(pl.multiple_of(start, 16), size), :]

    sends = []

    def send(src, b, start, size, dev, kind):
        copy = pltpu.make_async_remote_copy(
            src_ref=src,
            dst_ref=piece(b, start, size),
            send_sem=send_sem.at[b, kind],
            recv_sem=recv_sem.at[b, kind],
            device_id=dev,
            device_id_type=MESH,
        )
        copy.start()
        sends.append(copy)

    def arrived(b, start, size, kind):
        ref = piece(b, start, size)
        pltpu.make_async_remote_copy(
            src_ref=ref,
            dst_ref=ref,
            send_sem=send_sem.at[b, kind],
            recv_sem=recv_sem.at[b, kind],
            device_id=xdev,
            device_id_type=MESH,
        ).wait_recv()

    def load(src, dst, i):
        copy = pltpu.make_async_copy(src, dst, load_sem.at[i])
        copy.start()
        return copy

    barrier = pltpu.get_barrier_semaphore()
    for dev in (xdev, ydev, zdev, mdev):
        pl.semaphore_signal(barrier, inc=1, device_id=dev, device_id_type=MESH)
    pl.semaphore_wait(barrier, 4)

    for b in range(n_blocks):
        send(own_hbm(b, p * quarter, quarter), b, p * quarter, quarter, xdev, 0)
        send(own_hbm(b, pd * quarter, c1), b, pd * quarter, c1, xdev, 1)

    loads = [load(own_hbm(b, 0, depth), own.at[b], b) for b in range(n_blocks)]
    mem_load = load(mem_hbm, mem_v, n_blocks)
    lk_load = load(lk_hbm, lk_v, n_blocks + 1)
    lv_load = load(lv_hbm, lv_v, n_blocks + 2)

    def pass_quarter(b):
        if b >= n_blocks:
            return
        arrived(b, p * quarter, quarter, 0)
        src = piece(b, p * quarter, quarter)
        send(src, b, p * quarter, quarter, ydev, 2)
        send(src, b, p * quarter, quarter, zdev, 3)

    def pass_diagonal(b):
        if b >= n_blocks:
            return
        at_y = pz * quarter + c1
        arrived(b, pz * quarter, quarter, 3)
        send(piece(b, at_y, c2), b, at_y, c2, ydev, 4)
        at_z = py * quarter + c1 + c2
        arrived(b, py * quarter, quarter, 2)
        send(piece(b, at_z, c2), b, at_z, c2, zdev, 5)

    def complete(b):
        arrived(b, pd * quarter, c1, 1)
        arrived(b, pd * quarter + c1, c2, 4)
        arrived(b, pd * quarter + c1 + c2, c2, 5)

    def pump(b):
        pass_quarter(b)
        pass_diagonal(b - 1)

    mine = pl.ds(pl.multiple_of(f * depth, 128), depth)
    other = pl.ds(pl.multiple_of((1 - f) * depth, 128), depth)
    tile = 64

    @pl.loop(0, total // tile)
    def _(i):
        r = pl.ds(pl.multiple_of(i * tile, tile), tile)
        n = normalize(x_ref[r, :].astype(f32)).astype(bf16).astype(f32)
        n3 = n.reshape(tile // ROWS, ROWS, width)
        row = lax.broadcasted_iota(jnp.int32, n3.shape, 1)
        mean = jnp.sum(jnp.where(row < GROUP, n3, 0.0), axis=1, keepdims=True) * (1.0 / GROUP)
        n3 = jnp.where(row == frames, jnp.broadcast_to(mean, n3.shape), n3)
        rows_v[r, :] = n3.reshape(tile, width).astype(bf16)

    mem_load.wait()
    pass_quarter(0)
    pump(1)

    def project(b):
        loads[b].wait()
        complete(b)
        sums = matmul(rows_v[:, mine], own[b]) + matmul(rows_v[:, other], far[b])
        return sums.astype(bf16)

    def project_memory(b, target):
        step = 256

        @pl.loop(0, mem_v.shape[0] // step)
        def _(i):
            r = pl.ds(pl.multiple_of(i * step, step), step)
            sums = matmul(mem_v[r, mine], own[b]) + matmul(mem_v[r, other], far[b])
            target[r, :] = sums.astype(bf16)

    keys = project(0)
    ck_ref[...] = keys
    gk[...] = keys.astype(f32)
    project_memory(0, mk)
    pump(2)
    vals = project(1)
    cv_ref[...] = vals
    gv[...] = vals.astype(f32)
    project_memory(1, mv)
    pump(3)
    qs[...] = project(2).astype(f32)
    lk_load.wait()
    lv_load.wait()

    heads = cols // HD
    lanes3 = lax.broadcasted_iota(jnp.int32, (heads, ROWS, cols), 2)
    head3 = lax.broadcasted_iota(jnp.int32, (heads, ROWS, cols), 0)
    head_mask = jnp.where(lanes3 // HD == head3, 1.0, 0.0).astype(f32)
    row2 = lax.broadcasted_iota(jnp.int32, (heads * ROWS, KEYS), 0)
    lane2 = lax.broadcasted_iota(jnp.int32, (heads * ROWS, KEYS), 1)
    excluded = jnp.where((row2 % ROWS == frames) & (lane2 < mem_slots), -1.0, 0.0).astype(f32)
    pad8 = jnp.zeros((16 - ROWS, cols), f32)
    pad = jnp.zeros((KEYS - mem_slots - left_slots - 16, cols), bf16)
    scale = HD ** (-0.5)

    def gather_rows(mem_part, left_part, group_part, s):
        return jnp.concatenate(
            [
                mem_part[pl.ds(pl.multiple_of(s * mem_slots, mem_slots), mem_slots), :],
                left_part[s],
                jnp.concatenate(
                    [group_part[pl.ds(pl.multiple_of(s * ROWS, ROWS), ROWS), :], pad8], axis=0
                ).astype(bf16),
                pad,
            ],
            axis=0,
        )

    def attend(s):
        r = pl.ds(pl.multiple_of(s * ROWS, ROWS), ROWS)
        spread = (qs[r, :][None] * head_mask).reshape(heads * ROWS, cols).astype(bf16)
        k = gather_rows(mk, lk_v, gk, s)
        scores = (
            lax.dot_general(spread, k, (((1,), (1,)), ((), ())), preferred_element_type=f32) * scale
        )
        hide = bias_ref[pl.ds(s, 1), :] + excluded
        scores = jnp.where(hide < 0.0, masked_score, scores)
        top = jnp.max(scores, axis=-1, keepdims=True)
        e = jnp.exp(scores - top)
        probs = (e / jnp.sum(e, axis=-1, keepdims=True)).astype(bf16)
        v = gather_rows(mv, lv_v, gv, s)
        o = matmul(probs, v).reshape(heads, ROWS, cols) * head_mask
        att[r, :] = jnp.sum(o, axis=0)

    chunks = 4
    per_chunk = streams // chunks
    unroll = 4
    for c in range(chunks):

        @pl.loop(0, per_chunk // unroll)
        def _(i):
            for u in range(unroll):
                attend(c * per_chunk + i * unroll + u)

        if c < chunks - 1:
            pump(4 + c)

    def exchange(slot):
        copy = pltpu.make_async_remote_copy(
            src_ref=part.at[slot],
            dst_ref=peer.at[slot],
            send_sem=psend_sem.at[slot],
            recv_sem=precv_sem.at[slot],
            device_id=mdev,
            device_id_type=MESH,
        )
        copy.start()
        return copy

    loads[3].wait()
    complete(3)
    attended = att[...].astype(bf16)
    part[0, :, mine] = matmul(attended, own[3]).astype(bf16)
    part[0, :, other] = matmul(attended, far[3]).astype(bf16)
    first = exchange(0)
    pump(4 + chunks - 1)
    first.wait()

    wide = 16 * ROWS

    @pl.loop(0, total // wide)
    def _(i):
        r = pl.ds(pl.multiple_of(i * wide, wide), wide)
        a = part[0, r, :].astype(f32) + peer[0, r, :].astype(f32)
        a3 = a.reshape(wide // ROWS, ROWS, width)
        row = lax.broadcasted_iota(jnp.int32, a3.shape, 1)
        memory = jnp.sum(jnp.where(row == frames, a3, 0.0), axis=1)
        s = pl.ds(pl.multiple_of(i * 16, 16), 16)
        mnext_ref[s, :] = jnp.tanh(memory).astype(bf16)
        h = x_ref[r, :].astype(f32) + a
        hid[r, :] = h
        rows_v[r, :] = normalize(h).astype(bf16)

    ahead = 4 + chunks
    for j in range(n_ff):
        b = 4 + 2 * j
        pump(ahead)
        ahead += 1
        loads[b].wait()
        complete(b)
        up = matmul(rows_v[:, mine], own[b]) + matmul(rows_v[:, other], far[b])
        hbuf[...] = jax.nn.gelu(up, approximate=True).astype(bf16)
        if ahead <= n_blocks:
            pump(ahead)
            ahead += 1
        loads[b + 1].wait()
        complete(b + 1)
        near = matmul(hbuf[...], own[b + 1])
        away = matmul(hbuf[...], far[b + 1])
        if j == 0:
            dacc[:, mine] = near
            dacc[:, other] = away
        else:
            near = dacc[:, mine] + near
            away = dacc[:, other] + away
            if j < n_ff - 1:
                dacc[:, mine] = near
                dacc[:, other] = away
            else:
                part[1, :, mine] = near.astype(bf16)
                part[1, :, other] = away.astype(bf16)

    second = exchange(1)
    second.wait()

    @pl.loop(0, total // tile)
    def _(i):
        r = pl.ds(pl.multiple_of(i * tile, tile), tile)
        y = hid[r, :] + (part[1, r, :].astype(f32) + peer[1, r, :].astype(f32))
        out_ref[r, :] = (normalize(y) * gain_ref[...]).astype(bf16)

    for copy in sends:
        copy.wait_send()


def shards(
    features,
    memory_bank,
    memory_fill,
    left_keys,
    left_values,
    left_length,
    w_query,
    w_key,
    w_value,
    w_out,
    w_up,
    w_down,
    out_gain,
):
    frames, width_dev, all_streams = features.shape
    streams, mem_slots, width = memory_bank.shape
    left_slots = left_keys.shape[1]
    depth, cols = w_query.shape
    n_ff = w_up.shape[1] // cols
    n_blocks = 4 + 2 * n_ff
    total = streams * ROWS
    n_dp = lax.axis_size("dp")
    n_fsdp = lax.axis_size("fsdp")
    flattened = features.reshape(frames * width_dev, all_streams)
    arrived = lax.all_to_all(flattened, ("dp", "fsdp"), split_axis=1, concat_axis=0, tiled=True)
    arrived = arrived.reshape(n_dp * n_fsdp, frames, width_dev, streams)
    inputs = jnp.transpose(arrived, (3, 1, 0, 2)).reshape(streams, frames, width)
    x = jnp.pad(inputs, ((0, 0), (0, ROWS - frames), (0, 0))).reshape(total, width)
    slot = jnp.arange(KEYS, dtype=jnp.int32)[None, :]
    hidden_mem = (slot < mem_slots) & (slot < (mem_slots - memory_fill)[:, None])
    left_end = mem_slots + left_slots
    hidden_left = (
        (slot >= mem_slots)
        & (slot < left_end)
        & (slot - mem_slots < (left_slots - left_length)[:, None])
    )
    hidden = hidden_mem | hidden_left | (slot >= left_end + frames)
    bias = jnp.where(hidden, -1.0, 0.0).astype(f32)
    vmem = pl.BlockSpec(memory_space=pltpu.VMEM)
    hbm = pl.BlockSpec(memory_space=pl.ANY)
    out, mnext, ck, cv = pl.pallas_call(
        functools.partial(body, frames, mem_slots, left_slots),
        out_shape=(
            jax.ShapeDtypeStruct((total, width), bf16),
            jax.ShapeDtypeStruct((streams, width), bf16),
            jax.ShapeDtypeStruct((total, cols), bf16),
            jax.ShapeDtypeStruct((total, cols), bf16),
        ),
        in_specs=[vmem] * 3 + [hbm] * 9,
        out_specs=(vmem,) * 4,
        scratch_shapes=[
            pltpu.VMEM((n_blocks, depth, cols), bf16),
            pltpu.VMEM((n_blocks, depth, cols), bf16),
            pltpu.VMEM((streams * mem_slots, width), bf16),
            pltpu.VMEM(left_keys.shape, bf16),
            pltpu.VMEM(left_keys.shape, bf16),
            pltpu.VMEM((streams * mem_slots, cols), bf16),
            pltpu.VMEM((streams * mem_slots, cols), bf16),
            pltpu.VMEM((total, cols), f32),
            pltpu.VMEM((total, cols), f32),
            pltpu.VMEM((total, cols), f32),
            pltpu.VMEM((total, width), bf16),
            pltpu.VMEM((total, cols), f32),
            pltpu.VMEM((total, width), f32),
            pltpu.VMEM((total, cols), bf16),
            pltpu.VMEM((total, width), f32),
            pltpu.VMEM((2, total, width), bf16),
            pltpu.VMEM((2, total, width), bf16),
            pltpu.SemaphoreType.DMA((n_blocks, 6)),
            pltpu.SemaphoreType.DMA((n_blocks, 6)),
            pltpu.SemaphoreType.DMA((2,)),
            pltpu.SemaphoreType.DMA((2,)),
            pltpu.SemaphoreType.DMA((n_blocks + 3,)),
        ],
        compiler_params=pltpu.CompilerParams(
            collective_id=0, has_side_effects=True, vmem_limit_bytes=60 * 1024 * 1024
        ),
    )(
        x,
        bias,
        out_gain.reshape(1, width),
        memory_bank.reshape(streams * mem_slots, width),
        left_keys,
        left_values,
        w_query,
        w_key,
        w_value,
        w_out,
        w_up,
        w_down,
    )
    layer_out = out.reshape(streams, ROWS, width)[:, :frames]
    center_keys = ck.reshape(streams, ROWS, cols)[:, :GROUP]
    center_values = cv.reshape(streams, ROWS, cols)[:, :GROUP]
    return (layer_out, mnext, center_keys, center_values)


def solution(mesh):
    in_specs = (
        P(None, ("dp", "fsdp"), None),
        P(("dp", "fsdp"), None, None),
        P(("dp", "fsdp")),
        P(("dp", "fsdp"), None, "mp"),
        P(("dp", "fsdp"), None, "mp"),
        P(("dp", "fsdp")),
        P("fsdp", "mp"),
        P("fsdp", "mp"),
        P("fsdp", "mp"),
        P("mp", "fsdp"),
        P("fsdp", "mp"),
        P("mp", "fsdp"),
        P(),
    )
    out_specs = (
        P(("dp", "fsdp"), None, None),
        P(("dp", "fsdp"), None),
        P(("dp", "fsdp"), None, "mp"),
        P(("dp", "fsdp"), None, "mp"),
    )
    return jax.shard_map(shards, mesh=mesh, in_specs=in_specs, out_specs=out_specs, check_vma=False)
```

time: 238 us -> 106 us (0.45)
  waiting for transfers between devices: 94 us -> 11.9 us
  Pallas kernels: 0 us -> 71.5 us
  local copies, waits for them, and re-layouts: 56.7 us -> 12.4 us
  matrix products: 29.4 us -> 0 us
  blocking collectives: 17.6 us -> 0 us
  other arithmetic: 15.2 us -> 0.71 us
  between operations: 14.6 us -> 0.74 us
    pallas_call x0 -> x1, Pallas kernels: none -> 71.5 us  [shards(): pl.pallas_call(functools.partial(body, frames, mem_slots, left_slots), ou...]
    all_gather x5 -> x0, waiting for transfers between devices: 38.5 us -> none  [the longest x1 24.3 us: shards(): lax.all_gather(hidden, 'fsdp', axis=0, tiled=True)]
    psum x2 -> x0, waiting for transfers between devices: 29.5 us -> none  [the longest x1 18.5 us: shards(): lax.psum(attn_part.astype(jnp.bfloat16), 'mp').astype(jnp.float32)]
    dot_general x12 -> x0, matrix products: 29.4 us -> none  [the longest x6 15.5 us: matmul(): return jnp.dot(left, right, preferred_element_type=jnp.float32)]
    reshape x15 -> x2, local copies, waits for them, and re-layouts: 28 us -> 1.29 us  [the longest x1 0.9 us: shards(): jnp.pad(inputs, ((0, 0), (0, ROWS - frames), (0, 0))).reshape(total, width)]
    reduce_scatter x1 -> x0, waiting for transfers between devices: 23.3 us -> none  [shards(): lax.psum_scatter(matmul(halves, w_up).astype(jnp.bfloat16), 'fsdp', scatt...]
    all_to_all x2 -> x0, blocking collectives: 17.6 us -> none  [the longest x1 9.13 us: shards(): lax.all_to_all(h_norm, 'fsdp', split_axis=1, concat_axis=0, tiled=True)]
    all_to_all x1, waiting for transfers between devices: 0.01 us -> 11.9 us  [shards(): lax.all_to_all(flattened, ('dp', 'fsdp'), split_axis=1, concat_axis=0, ti...]
  transfers between devices with their start and end apart: 9 -> 1, of which waited for: 7 -> 1; matrix products, arithmetic and copies ran while one was open for 32% -> 1% of each run, Pallas kernels for 0% -> 0%
where the time goes in v1:
time: 106 us; the launch traced here: 105 us
  Pallas kernels  71.5 us (67%)
  local copies, waits for them, and re-layouts  12.4 us (12%)
  waiting for transfers between devices  11.9 us (11%)
  starting transfers between devices  8.34 us (8%)
    pallas_call x1, Pallas kernels, shards(): pl.pallas_call(functools.partial(body, frames, mem_slots, left_slots), ou...  71.5 us
    all_to_all x1, waiting for transfers between devices, shards(): lax.all_to_all(flattened, ('dp', 'fsdp'), split_axis=1, concat_axis=0, ti...  11.9 us
    all_to_all x1, starting transfers between devices, shards(): lax.all_to_all(flattened, ('dp', 'fsdp'), split_axis=1, concat_axis=0, ti...  8.34 us
    unnamed x9, local copies, waits for them, and re-layouts  6.49 us
  transfers between devices with their start and end apart: 1, of which 1 were waited for; matrix products, arithmetic and copies ran while one was open for 1% of the time, Pallas kernels for 0%

profile of v1, /device:TPU:0, one launch (start us, length us, event | category | flops | bytes accessed | tf_op | source)
XLA Modules:
  0.0 105.5 jit_solution(16889732711811337938)
XLA Ops:
  0.6 0.0 copy-start
  0.6 0.0 copy-start.1
  0.7 1.8 %copy.23 = bf16[5,64,512]{1,0,2:T(8,128)(2,1)S(1)} copy(bf16[5,64,512]{2,1,0:T(8,128)(2,1)} %param.13) | data formatting | bytes 655360 | tf_op args[0]
  2.4 1.3 %all_to_all.12 = bf16[320,16,32]{0,2,1:T(8,128)(2,1)} reshape(bf16[5,64,512]{1,0,2:T(8,128)(2,1)S(1)} %copy.23) | data formatting | bytes 655360 | tf_op jit(solution)/shard_map/all_to_all | solution.py:383
  3.7 8.3 %all-to-all-start = ((bf16[320,16,32]{0,2,1:T(8,128)(2,1)}), bf16[320,16,32]{0,2,1:T(8,128)(2,1)S(1)}, u32[]{:S(2)}, u32[]{:S(2)}) async-start(bf16[320,16,32]{0,2,1:T(8,128)(2,1)} %all_to_all.12), calls=%async_computation | async-start | bytes 786432 | tf_op jit(solution)/shard_map/all_to_all | solution.py:383
  12.1 0.0 copy-done
  12.1 0.0 copy-done.1
  12.2 0.7 fusion.3.bias_ref
  12.8 11.9 %all-to-all-done = bf16[320,16,32]{0,2,1:T(8,128)(2,1)S(1)} async-done(((bf16[320,16,32]{0,2,1:T(8,128)(2,1)}), bf16[320,16,32]{0,2,1:T(8,128)(2,1)S(1)}, u32[]{:S(2)}, u32[]{:S(2)}) %all-to-all-start) | async-done | bytes 327712 | tf_op jit(solution)/shard_map/all_to_all | solution.py:383
  24.7 0.4 reshape.66
  25.1 0.8 copy.29
  25.9 0.5 reshape.74
  26.4 0.9 pad_bitcast_fusion.x_ref
  27.3 71.5 %shard_map.156 = (bf16[256,1024]{1,0:T(8,128)(2,1)}, bf16[32,1024]{1,0:T(8,128)(2,1)}, bf16[256,512]{1,0:T(8,128)(2,1)}, bf16[256,512]{1,0:T(8,128)(2,1)}) custom-call(bf16[256,1024]{1,0:T(8,128)(2,1)} %pad_bitcast_fusion.x_ref, f32[32,128]{1,0:T(8,128)} %fusion.3.bias_ref, f32[1,1024]{1,0:T(1,128)} %bitcast.22, bf16[1024,1024]{1,0:T(8,128)(2,1)} %bitcast.17, ...), custom_call_target="tpu_custom_call" | custom-call | tf_op jit(solution)/shard_map/pallas_call | solution.py:399
  98.8 2.0 %copy.27 = bf16[32,5,1024]{2,0,1:T(8,128)(2,1)} copy(bf16[32,5,1024]{2,1,0:T(8,128)(2,1)} %bitcast.19) | data formatting | bytes 655360
  100.7 1.6 %slice.13 = bf16[32,4,512]{2,1,0:T(4,128)(2,1)} slice(bf16[32,8,512]{2,1,0:T(8,128)(2,1)} %bitcast.21), slice={[0:32], [0:4], [0:512]} | slice | bytes 262144 | tf_op jit(solution)/shard_map/slice | solution.py:451
  102.4 1.6 %slice.14 = bf16[32,4,512]{2,1,0:T(4,128)(2,1)} slice(bf16[32,8,512]{2,1,0:T(8,128)(2,1)} %bitcast.20), slice={[0:32], [0:4], [0:512]} | slice | bytes 262144 | tf_op jit(solution)/shard_map/slice | solution.py:452
  104.0 1.5 %copy.32 = bf16[32,1024]{1,0:T(8,128)(2,1)} copy(bf16[32,1024]{1,0:T(8,128)(2,1)} %get-tuple-element.21) | data formatting | bytes 131072
  (4 shorter events, 0.0 us)
Async XLA Ops:
  0.6 11.5 %copy-start = (s32[32]{0:T(128)S(1)}, s32[32]{0:T(128)}, u32[]{:S(2)}) copy-start(s32[32]{0:T(128)} %param.18) | copy-start | bytes 388
  0.6 11.5 %copy-start.1 = (s32[32]{0:T(128)S(1)}, s32[32]{0:T(128)}, u32[]{:S(2)}) copy-start(s32[32]{0:T(128)} %param.15) | copy-start | bytes 388
  3.7 21.0 %all-to-all-start = ((bf16[320,16,32]{0,2,1:T(8,128)(2,1)}), bf16[320,16,32]{0,2,1:T(8,128)(2,1)S(1)}, u32[]{:S(2)}, u32[]{:S(2)}) async-start(bf16[320,16,32]{0,2,1:T(8,128)(2,1)} %all_to_all.12), calls=%async_computation | async-start | bytes 786432 | tf_op jit(solution)/shard_map/all_to_all | solution.py:383

commit v2 on v1

--- a/solution.py
+++ b/solution.py
@@ -34,8 +34,10 @@
     frames,
     mem_slots,
     left_slots,
-    x_ref,
-    bias_ref,
+    packed,
+    f_ref,
+    fill_ref,
+    length_ref,
     gain_ref,
     mem_hbm,
     lk_hbm,
@@ -50,6 +52,9 @@
     mnext_ref,
     ck_ref,
     cv_ref,
+    x_ref,
+    outbox,
+    inbox,
     far,
     own,
     mem_v,
@@ -72,6 +77,8 @@
     psend_sem,
     precv_sem,
     load_sem,
+    fsend_sem,
+    frecv_sem,
 ):
     d = lax.axis_index("dp")
     m = lax.axis_index("mp")
@@ -136,14 +143,54 @@
         copy.start()
         return copy
 
+    peers = inbox.shape[0] if packed else 0
+    n_fsdp = lax.axis_size("fsdp")
+    me = d * n_fsdp + f
+
+    def place(offset):
+        return lax.rem(me + offset, peers)
+
+    def device_of(index):
+        return (lax.div(index, n_fsdp), m, lax.rem(index, n_fsdp))
+
     barrier = pltpu.get_barrier_semaphore()
-    for dev in (xdev, ydev, zdev, mdev):
+    greeted = [device_of(place(o)) for o in range(1, peers)] if packed else [xdev, ydev, zdev]
+    greeted.append(mdev)
+    for dev in greeted:
         pl.semaphore_signal(barrier, inc=1, device_id=dev, device_id_type=MESH)
-    pl.semaphore_wait(barrier, 4)
-
-    for b in range(n_blocks):
+
+    if packed:
+        pairs = outbox.shape[1]
+        for k in range(pairs):
+            low = f_ref[2 * k].astype(f32)
+            high = f_ref[min(2 * k + 1, frames - 1)].astype(f32)
+            turned = jnp.concatenate([low, high], axis=0).T.astype(bf16)
+            outbox[:, k] = turned.reshape(peers, streams, turned.shape[1])
+
+    pl.semaphore_wait(barrier, len(greeted))
+
+    fsends = []
+    for o in range(1, peers):
+        copy = pltpu.make_async_remote_copy(
+            src_ref=outbox.at[place(o)],
+            dst_ref=inbox.at[me],
+            send_sem=fsend_sem.at[o],
+            recv_sem=frecv_sem.at[o],
+            device_id=device_of(place(o)),
+            device_id_type=MESH,
+        )
+        copy.start()
+        fsends.append(copy)
+
+    def send_own(b):
+        if b >= n_blocks:
+            return
         send(own_hbm(b, p * quarter, quarter), b, p * quarter, quarter, xdev, 0)
         send(own_hbm(b, pd * quarter, c1), b, pd * quarter, c1, xdev, 1)
+
+    lead = 3
+    for b in range(lead):
+        send_own(b)
 
     loads = [load(own_hbm(b, 0, depth), own.at[b], b) for b in range(n_blocks)]
     mem_load = load(mem_hbm, mem_v, n_blocks)
@@ -154,6 +201,7 @@
         if b >= n_blocks:
             return
         arrived(b, p * quarter, quarter, 0)
+        send_own(b + lead)
         src = piece(b, p * quarter, quarter)
         send(src, b, p * quarter, quarter, ydev, 2)
         send(src, b, p * quarter, quarter, zdev, 3)
@@ -180,6 +228,36 @@
     mine = pl.ds(pl.multiple_of(f * depth, 128), depth)
     other = pl.ds(pl.multiple_of((1 - f) * depth, 128), depth)
     tile = 64
+
+    if packed:
+        inbox[pl.ds(me, 1)] = outbox[pl.ds(me, 1)]
+        for o in range(1, peers):
+            ref = inbox.at[lax.rem(me + peers - o, peers)]
+            pltpu.make_async_remote_copy(
+                src_ref=ref,
+                dst_ref=ref,
+                send_sem=fsend_sem.at[o],
+                recv_sem=frecv_sem.at[o],
+                device_id=xdev,
+                device_id_type=MESH,
+            ).wait_recv()
+        half = inbox.shape[3] // 2
+        parts = []
+        for t in range(frames):
+            k, side = t // 2, t % 2
+            lanes = slice(side * half, side * half + half)
+            parts.append(
+                jnp.concatenate([inbox[i, k][:, lanes] for i in range(peers)], axis=1)
+            )
+        major = jnp.concatenate(parts, axis=0)
+    else:
+        major = f_ref[...]
+    count = frames * streams
+    r_id = lax.broadcasted_iota(jnp.int32, (total, count), 0)
+    c_id = lax.broadcasted_iota(jnp.int32, (total, count), 1)
+    frame_id = r_id % ROWS
+    target = jnp.where(frame_id < frames, frame_id * streams + r_id // ROWS, -1)
+    x_ref[...] = matmul(jnp.where(target == c_id, 1.0, 0.0).astype(bf16), major).astype(bf16)
 
     @pl.loop(0, total // tile)
     def _(i):
@@ -231,6 +309,8 @@
     row2 = lax.broadcasted_iota(jnp.int32, (heads * ROWS, KEYS), 0)
     lane2 = lax.broadcasted_iota(jnp.int32, (heads * ROWS, KEYS), 1)
     excluded = jnp.where((row2 % ROWS == frames) & (lane2 < mem_slots), -1.0, 0.0).astype(f32)
+    lane1 = lax.broadcasted_iota(jnp.int32, (1, KEYS), 1)
+    left_end = mem_slots + left_slots
     pad8 = jnp.zeros((16 - ROWS, cols), f32)
     pad = jnp.zeros((KEYS - mem_slots - left_slots - 16, cols), bf16)
     scale = HD ** (-0.5)
@@ -255,7 +335,12 @@
         scores = (
             lax.dot_general(spread, k, (((1,), (1,)), ((), ())), preferred_element_type=f32) * scale
         )
-        hide = bias_ref[pl.ds(s, 1), :] + excluded
+        first_mem = mem_slots - fill_ref[s]
+        first_left = left_end - length_ref[s]
+        first = jnp.where(lane1 < mem_slots, first_mem, first_left)
+        first = jnp.where(lane1 < left_end, first, 0)
+        hide1 = (lane1 < first) | (lane1 >= left_end + frames)
+        hide = jnp.where(hide1, -1.0, 0.0) + excluded
         scores = jnp.where(hide < 0.0, masked_score, scores)
         top = jnp.max(scores, axis=-1, keepdims=True)
         e = jnp.exp(scores - top)
@@ -351,8 +436,23 @@
         y = hid[r, :] + (part[1, r, :].astype(f32) + peer[1, r, :].astype(f32))
         out_ref[r, :] = (normalize(y) * gain_ref[...]).astype(bf16)
 
-    for copy in sends:
+    for copy in sends + fsends:
         copy.wait_send()
+
+
+def finish(frames, rows_ref, mem_ref, keys_ref, vals_ref, out_ref, mnext_ref, ck_ref, cv_ref):
+    total, width = rows_ref.shape
+    streams = total // ROWS
+    count = frames * streams
+    r_id = lax.broadcasted_iota(jnp.int32, (count, total), 0)
+    c_id = lax.broadcasted_iota(jnp.int32, (count, total), 1)
+    pick = (r_id % streams) * ROWS + r_id // streams
+    moved = matmul(jnp.where(pick == c_id, 1.0, 0.0).astype(bf16), rows_ref[...])
+    out_ref[...] = moved.astype(bf16)
+    mnext_ref[...] = mem_ref[...]
+    for src, dst in ((keys_ref, ck_ref), (vals_ref, cv_ref)):
+        values = src[...].astype(f32).reshape(streams, ROWS, src.shape[1])
+        dst[...] = values[:, :GROUP].astype(bf16)
 
 
 def shards(
@@ -379,34 +479,33 @@
     total = streams * ROWS
     n_dp = lax.axis_size("dp")
     n_fsdp = lax.axis_size("fsdp")
-    flattened = features.reshape(frames * width_dev, all_streams)
-    arrived = lax.all_to_all(flattened, ("dp", "fsdp"), split_axis=1, concat_axis=0, tiled=True)
-    arrived = arrived.reshape(n_dp * n_fsdp, frames, width_dev, streams)
-    inputs = jnp.transpose(arrived, (3, 1, 0, 2)).reshape(streams, frames, width)
-    x = jnp.pad(inputs, ((0, 0), (0, ROWS - frames), (0, 0))).reshape(total, width)
-    slot = jnp.arange(KEYS, dtype=jnp.int32)[None, :]
-    hidden_mem = (slot < mem_slots) & (slot < (mem_slots - memory_fill)[:, None])
-    left_end = mem_slots + left_slots
-    hidden_left = (
-        (slot >= mem_slots)
-        & (slot < left_end)
-        & (slot - mem_slots < (left_slots - left_length)[:, None])
-    )
-    hidden = hidden_mem | hidden_left | (slot >= left_end + frames)
-    bias = jnp.where(hidden, -1.0, 0.0).astype(f32)
+    peers = n_dp * n_fsdp
+    packed = 2 * width_dev == KEYS and streams % 16 == 0
+    if packed:
+        feed = features
+    else:
+        flat = features.reshape(frames * width_dev, all_streams)
+        got = lax.all_to_all(flat, ("dp", "fsdp"), split_axis=1, concat_axis=0, tiled=True)
+        got = got.reshape(peers, frames, width_dev, streams)
+        feed = jnp.transpose(got, (1, 3, 0, 2)).reshape(frames * streams, width)
+    slots = (peers, (frames + 1) // 2, streams, KEYS) if packed else (1, 1, 16, KEYS)
     vmem = pl.BlockSpec(memory_space=pltpu.VMEM)
     hbm = pl.BlockSpec(memory_space=pl.ANY)
+    smem = pl.BlockSpec(memory_space=pltpu.SMEM)
     out, mnext, ck, cv = pl.pallas_call(
-        functools.partial(body, frames, mem_slots, left_slots),
+        functools.partial(body, frames, mem_slots, left_slots, packed),
         out_shape=(
             jax.ShapeDtypeStruct((total, width), bf16),
             jax.ShapeDtypeStruct((streams, width), bf16),
             jax.ShapeDtypeStruct((total, cols), bf16),
             jax.ShapeDtypeStruct((total, cols), bf16),
         ),
-        in_specs=[vmem] * 3 + [hbm] * 9,
+        in_specs=[vmem, smem, smem, vmem] + [hbm] * 9,
         out_specs=(vmem,) * 4,
         scratch_shapes=[
+            pltpu.VMEM((total, width), bf16),
+            pltpu.VMEM(slots, bf16),
+            pltpu.VMEM(slots, bf16),
             pltpu.VMEM((n_blocks, depth, cols), bf16),
             pltpu.VMEM((n_blocks, depth, cols), bf16),
             pltpu.VMEM((streams * mem_slots, width), bf16),
@@ -429,13 +528,16 @@
             pltpu.SemaphoreType.DMA((2,)),
             pltpu.SemaphoreType.DMA((2,)),
             pltpu.SemaphoreType.DMA((n_blocks + 3,)),
+            pltpu.SemaphoreType.DMA((peers,)),
+            pltpu.SemaphoreType.DMA((peers,)),
         ],
         compiler_params=pltpu.CompilerParams(
             collective_id=0, has_side_effects=True, vmem_limit_bytes=60 * 1024 * 1024
         ),
     )(
-        x,
-        bias,
+        feed,
+        memory_fill,
+        left_length,
         out_gain.reshape(1, width),
         memory_bank.reshape(streams * mem_slots, width),
         left_keys,
@@ -447,10 +549,19 @@
         w_up,
         w_down,
     )
-    layer_out = out.reshape(streams, ROWS, width)[:, :frames]
-    center_keys = ck.reshape(streams, ROWS, cols)[:, :GROUP]
-    center_values = cv.reshape(streams, ROWS, cols)[:, :GROUP]
-    return (layer_out, mnext, center_keys, center_values)
+    layer_out, memory_next, center_keys, center_values = pl.pallas_call(
+        functools.partial(finish, frames),
+        out_shape=(
+            jax.ShapeDtypeStruct((frames * streams, width), bf16),
+            jax.ShapeDtypeStruct((streams, width), bf16),
+            jax.ShapeDtypeStruct((streams, GROUP, cols), bf16),
+            jax.ShapeDtypeStruct((streams, GROUP, cols), bf16),
+        ),
+        in_specs=[vmem] * 4,
+        out_specs=(vmem,) * 4,
+    )(out, mnext, ck, cv)
+    layer_out = jnp.transpose(layer_out.reshape(frames, streams, width), (1, 0, 2))
+    return (layer_out, memory_next, center_keys, center_values)
 
 
 def solution(mesh):

time: 106 us -> 87.4 us (0.82)
  Pallas kernels: 71.5 us -> 86.6 us
  local copies, waits for them, and re-layouts: 12.4 us -> 0 us
  waiting for transfers between devices: 11.9 us -> 0 us
  starting transfers between devices: 8.34 us -> 0 us
    pallas_call x1 -> x2, Pallas kernels: 71.5 us -> 86.6 us  [the longest x1 84.4 us: shards(): pl.pallas_call(functools.partial(body, frames, mem_slots, left_slots, pac...]
    all_to_all x1 -> x0, waiting for transfers between devices: 11.9 us -> none  [shards(): lax.all_to_all(flattened, ('dp', 'fsdp'), split_axis=1, concat_axis=0, ti...]
    all_to_all x1 -> x0, starting transfers between devices: 8.34 us -> none  [shards(): lax.all_to_all(flattened, ('dp', 'fsdp'), split_axis=1, concat_axis=0, ti...]
    unnamed x9 -> x0, local copies, waits for them, and re-layouts: 6.49 us -> none
    slice x2 -> x0, local copies, waits for them, and re-layouts: 3.28 us -> none  [the longest x1 1.64 us: shards(): center_keys = ck.reshape(streams, ROWS, cols)[:, :GROUP]]
    all_to_all x1 -> x0, local copies, waits for them, and re-layouts: 1.32 us -> none  [shards(): lax.all_to_all(flattened, ('dp', 'fsdp'), split_axis=1, concat_axis=0, ti...]
    reshape x2 -> x0, local copies, waits for them, and re-layouts: 1.29 us -> none  [the longest x1 0.9 us: shards(): jnp.pad(inputs, ((0, 0), (0, ROWS - frames), (0, 0))).reshape(total, width)]
  transfers between devices with their start and end apart: 1 -> 0, of which waited for: 1 -> 0; matrix products, arithmetic and copies ran while one was open for 1% -> 0% of each run, Pallas kernels for 0% -> 0%
where the time goes in v2:
time: 87.4 us; the launch traced here: 87.2 us
  Pallas kernels  86.6 us (99%)
    pallas_call x1, Pallas kernels, shards(): pl.pallas_call(functools.partial(body, frames, mem_slots, left_slots, pac...  84.4 us
    pallas_call x1, Pallas kernels, shards(): pl.pallas_call(functools.partial(finish, frames), out_shape=(jax.ShapeDty...  2.24 us

profile of v2, /device:TPU:0, one launch (start us, length us, event | category | flops | bytes accessed | tf_op | source)
XLA Modules:
  0.0 87.2 jit_solution(4153380937306748438)
XLA Ops:
  0.6 84.4 %shard_map.156 = (bf16[256,1024]{1,0:T(8,128)(2,1)}, bf16[32,1024]{1,0:T(8,128)(2,1)}, bf16[256,512]{1,0:T(8,128)(2,1)}, bf16[256,512]{1,0:T(8,128)(2,1)}) custom-call(bf16[5,64,512]{2,1,0:T(8,128)(2,1)} %f_ref.1, s32[32]{0:T(128)} %fill_ref.1, s32[32]{0:T(128)} %length_ref.1, f32[1,1024]{1,0:T(1,128)} %bitcast.6, bf16[1024,1024]{1,0:T(8,128)(2,1)} %bitcast.5, ...), custom_call_target="tpu_custom_call" | custom-call | tf_op jit(solution)/shard_map/pallas_call | solution.py:495
  85.0 2.2 %shard_map.157 = (bf16[160,1024]{1,0:T(8,128)(2,1)}, bf16[32,1024]{1,0:T(8,128)(2,1)}, bf16[32,4,512]{2,1,0:T(4,128)(2,1)}, bf16[32,4,512]{2,1,0:T(4,128)(2,1)}) custom-call(bf16[256,1024]{1,0:T(8,128)(2,1)} %get-tuple-element.12.rows_ref, bf16[32,1024]{1,0:T(8,128)(2,1)} %get-tuple-element.13.mem_ref, bf16[256,512]{1,0:T(8,128)(2,1)} %get-tuple-element.14.keys_ref, ...), custom_call_target="tpu_custom_call" | custom-call | tf_op jit(solution)/shard_map/pallas_call | solution.py:552
